TPU v7x, 32 devices: a whole 2x2x4 slice. The times are simulated.
32 devices in a mesh: comp: 8 (over z, core), blk: 4 (over y, x).
Axes of the slice: x: 2, y: 2, z: 4, core: 2. Of those that a mesh axis runs over, the one named last changes fastest.
Arguments:
- state_now: float32 [8, 6, 32, 32, 256], P('comp', None, 'blk'), may hold values from -5 to 5
- state_prev: float32 [8, 6, 32, 32, 256], P('comp', None, 'blk'), may hold values from -5 to 5
- viscosity: float32 [8, 32, 32, 256], P('comp', 'blk'), may hold values from 0.05 to 0.5
- jacobian: float32 [8, 3, 6, 6], P('comp'), may hold values from -0.4 to 0.4
- donor_cell: int32 [8, 4, 8, 2, 8, 128], P('comp', 'blk'), may hold values from 0 to 57343, as said below
- interp_weight: float32 [8, 4, 8, 2, 8, 128], P('comp', 'blk'), may hold values from 0 to 1
- recv_cell: int32 [8, 4, 8, 2, 128], P('comp', 'blk'), may hold values from 0 to 57343, as said below
- pair_tiles: int32 [4, 8, 8], P('blk'), may hold values from 0 to 2, as said below
Outputs:
- state_next: float32 [8, 6, 32, 32, 256], P('comp', None, 'blk')
Inputs may be any that keep to these rules, and one draw needn't show every extreme that they name: `donor_cell`: the cells of one donor tile point are the eight corners of a cube of adjacent cells, corner k = 4 i + 2 j + l offset by (i, j, l). `recv_cell`: the receiving cells of one device are all different. `pair_tiles`: for each block index some destination component takes 2 tiles from every source component.
All inputs are finite; a program needn't handle non-finite values.
Results may differ from a plain program's by a relative error of at most 0.0003.
Values sent between devices are 32-bit elements; how exact they have to be, the bound alone decides.
A program may use at most 128 MiB of HBM per device.

v0:
```python
import functools

import jax
import jax.numpy as jnp
from jax import lax
from jax.experimental import pallas as pl
from jax.experimental.pallas import tpu as pltpu
from jax.sharding import PartitionSpec as P

SUBITERS = 2


time_scale = 0.5
pseudo_diag = 2.5

MESH = pl.DeviceIdType.MESH
VMEM_LIMIT = 60 * 1024 * 1024
F32 = jnp.float32
BF16 = jnp.bfloat16


def split(value):
    high = value.astype(BF16)
    low = (value - high.astype(F32)).astype(BF16)
    return high, low


def fill_mix(jac_ref, mix_hi, mix_lo, nvar, width_y):
    columns = mix_hi.shape[1]
    row = lax.broadcasted_iota(jnp.int32, (width_y, columns), 0)
    col = lax.broadcasted_iota(jnp.int32, (width_y, columns), 1)
    for v in range(nvar):
        block = jnp.zeros((width_y, columns), F32)
        for d in range(3):
            for w in range(nvar):
                block = jnp.where(col == row + (d * nvar + w) * width_y, 0.5 * jac_ref[d, v, w], block)
        high, low = split(block)
        mix_hi[v * width_y : (v + 1) * width_y, :] = high
        mix_lo[v * width_y : (v + 1) * width_y, :] = low


def flux_plane(centre, below, above, kappa, mix_hi, mix_lo):
    shape = centre.shape
    nvar, width_y, width_z = shape
    flat = centre.reshape(nvar * width_y, width_z)
    at_y = lax.broadcasted_iota(jnp.int32, shape, 1)
    at_z = lax.broadcasted_iota(jnp.int32, shape, 2)

    def moved(shift, axis, keep):
        return jnp.where(keep, pltpu.roll(flat, shift, axis).reshape(shape), 0.0)

    next_y = moved(nvar * width_y - 1, 0, at_y < width_y - 1)
    last_y = moved(1, 0, at_y > 0)
    next_z = moved(width_z - 1, 1, at_z < width_z - 1)
    last_z = moved(1, 1, at_z > 0)
    beside = (above + below) + (next_y + last_y) + (next_z + last_z)
    diffs = [above - below, next_y - last_y, next_z - last_z]
    diffs = jnp.concatenate([d.reshape(flat.shape) for d in diffs], axis=0)
    high, low = split(diffs)
    hi = mix_hi[...]
    convect = jnp.dot(hi, high, preferred_element_type=F32)
    convect += jnp.dot(mix_lo[...], high, preferred_element_type=F32)
    convect += jnp.dot(hi, low, preferred_element_type=F32)
    return convect.reshape(shape) + kappa[None] * (6.0 * centre - beside)


def comp_copies(comps, source_ref, landing, send_sem, recv_sem):
    mine = lax.axis_index("comp")

    def copy(d):
        peer = lax.rem(mine + d, comps)
        return pltpu.make_async_remote_copy(
            src_ref=source_ref.at[peer], dst_ref=landing.at[d],
            send_sem=send_sem.at[d], recv_sem=recv_sem.at[d],
            device_id={"comp": peer}, device_id_type=MESH,
        )

    return mine, copy


def greet_comps(comps, barrier):
    mine = lax.axis_index("comp")
    for d in range(1, comps):
        peer = lax.rem(mine + d, comps)
        pl.semaphore_signal(barrier, inc=1, device_id={"comp": peer}, device_id_type=MESH)


def relax_kernel(count, comps, jac_ref, state_ref, now_ref, prev_ref, kappa_ref, *refs):
    if comps:
        weight_ref, out_ref, held_ref = refs[:3]
        landing, weight_send, weight_recv = refs[-3:]
        refs = refs[3:-3]
    else:
        out_ref = refs[0]
        refs = refs[1:]
    halo, rstar, first, second, mix_hi, mix_lo, send_sem, recv_sem = refs
    me = lax.axis_index("blk")
    right = lax.rem(me + 1, count)
    left = lax.rem(me + count - 1, count)
    has_left = me > 0
    has_right = me < count - 1
    nvar, rows, width_y, width_z = state_ref.shape
    barrier = pltpu.get_barrier_semaphore()

    @pl.when(has_left)
    def _():
        pl.semaphore_signal(barrier, inc=1, device_id={"blk": left}, device_id_type=MESH)

    @pl.when(has_right)
    def _():
        pl.semaphore_signal(barrier, inc=1, device_id={"blk": right}, device_id_type=MESH)

    if comps:
        greet_comps(comps, barrier)

    @pl.when(jnp.logical_not(has_left))
    def _():
        for k in range(3):
            halo[k, 0] = jnp.zeros((nvar, width_y, width_z), F32)

    @pl.when(jnp.logical_not(has_right))
    def _():
        for k in range(3):
            halo[k, 1] = jnp.zeros((nvar, width_y, width_z), F32)

    peers = has_left.astype(jnp.int32) + has_right.astype(jnp.int32)
    pl.semaphore_wait(barrier, peers + max(comps - 1, 0))

    fields = [state_ref, first, second]

    def to_left(k):
        return pltpu.make_async_remote_copy(
            src_ref=fields[k].at[:, 0], dst_ref=halo.at[k, 1],
            send_sem=send_sem.at[k, 1], recv_sem=recv_sem.at[k, 1],
            device_id={"blk": left}, device_id_type=MESH,
        )

    def to_right(k):
        return pltpu.make_async_remote_copy(
            src_ref=fields[k].at[:, rows - 1], dst_ref=halo.at[k, 0],
            send_sem=send_sem.at[k, 0], recv_sem=recv_sem.at[k, 0],
            device_id={"blk": right}, device_id_type=MESH,
        )

    def start(k):
        @pl.when(has_left)
        def _():
            to_left(k).start()

        @pl.when(has_right)
        def _():
            to_right(k).start()

    def arrive(k):
        @pl.when(has_left)
        def _():
            to_right(k).wait_recv()

        @pl.when(has_right)
        def _():
            to_left(k).wait_recv()

    def plane(k, x, below, above):
        kappa = kappa_ref[x]
        centre = fields[k][:, x]
        flow = flux_plane(centre, below, above, kappa, mix_hi, mix_lo)
        scale = -1.0 / (pseudo_diag + 6.0 * kappa)
        if k == 0:
            base = time_scale * (3.0 * centre - 4.0 * now_ref[:, x] + prev_ref[:, x]) + flow
            rstar[:, x] = base
            first[:, x] = base * scale[None]
        else:
            step = (rstar[:, x] + flow - 6.0 * kappa[None] * centre) * scale[None]
            if k == 1:
                second[:, x] = step
            else:
                out_ref[:, x] = state_ref[:, x] + step

    start(0)
    if comps:
        mine, copy = comp_copies(comps, weight_ref, landing, weight_send, weight_recv)
        for d in range(1, comps):
            copy(d).start()
        held_ref[mine] = weight_ref[mine]
    fill_mix(jac_ref, mix_hi, mix_lo, nvar, width_y)
    for k in range(3):
        field = fields[k]

        def inner(x, carry, k=k, field=field):
            plane(k, x, field[:, x - 1], field[:, x + 1])
            return carry

        lax.fori_loop(1, rows - 1, inner, 0)
        arrive(k)
        plane(k, 0, halo[k, 0], field[:, 1])
        plane(k, rows - 1, field[:, rows - 2], halo[k, 1])
        if k < 2:
            start(k + 1)
    if comps:
        for d in range(1, comps):
            copy(d).wait()
            held_ref[lax.rem(mine - d + comps, comps)] = landing[d]
    for k in range(3):
        @pl.when(has_left)
        def _(k=k):
            to_left(k).wait_send()

        @pl.when(has_right)
        def _(k=k):
            to_right(k).wait_send()


def relax(jac, state, now, prev, kappa, weights=None):
    count = lax.axis_size("blk")
    nvar, rows, width_y, width_z = state.shape
    vmem = pl.BlockSpec(memory_space=pltpu.VMEM)
    whole = pltpu.VMEM(state.shape, F32)
    mixed = pltpu.VMEM((nvar * width_y, 3 * nvar * width_y), BF16)
    operands = [jac, state, now, prev, kappa]
    outs = [jax.ShapeDtypeStruct(state.shape, F32)]
    scratch = [
        pltpu.VMEM((3, 2, nvar, width_y, width_z), F32),
        whole, whole, whole, mixed, mixed,
        pltpu.SemaphoreType.DMA((3, 2)),
        pltpu.SemaphoreType.DMA((3, 2)),
    ]
    comps = 0
    if weights is not None:
        comps = weights.shape[0]
        operands.append(weights)
        outs.append(jax.ShapeDtypeStruct(weights.shape, F32))
        scratch += [
            pltpu.VMEM(weights.shape, F32),
            pltpu.SemaphoreType.DMA((comps,)),
            pltpu.SemaphoreType.DMA((comps,)),
        ]
    return pl.pallas_call(
        functools.partial(relax_kernel, count, comps),
        out_shape=outs,
        in_specs=[pl.BlockSpec(memory_space=pltpu.SMEM)] + [vmem] * (len(operands) - 1),
        out_specs=[vmem] * len(outs),
        scratch_shapes=scratch,
        compiler_params=pltpu.CompilerParams(
            collective_id=0 if comps else 1, has_side_effects=True, vmem_limit_bytes=VMEM_LIMIT
        ),
        name="relax",
    )(*operands)


def gather_kernel(strides, live_ref, state_ref, base_ref, weight_ref, out_ref, packed):
    nvar, pairs, width_z = state_ref.shape
    width_y, shift = strides
    tiles, _, tile = base_ref.shape
    for v in range(nvar):
        high, low = split(state_ref[v])
        packed[v * pairs : (v + 1) * pairs, :width_z] = high
        packed[v * pairs : (v + 1) * pairs, width_z:] = low

    def one(t, carry):
        @pl.when(live_ref[t] > 0)
        def _():
            base = base_ref[t]
            pair = lax.shift_right_logical(base, shift)
            depth = jnp.bitwise_and(base, width_z - 1)
            depth = jnp.concatenate([depth, depth + 1], axis=1)
            pair = jnp.concatenate([pair, pair], axis=1)
            at_z = lax.broadcasted_iota(jnp.int32, (width_z, 2 * tile), 0)
            hot = jnp.where(at_z == depth, 1.0, 0.0).astype(BF16)
            hot = jnp.concatenate([hot, hot], axis=0)
            found = jnp.dot(packed[...], hot, preferred_element_type=F32)
            at_pair = lax.broadcasted_iota(jnp.int32, (pairs, 2 * tile), 0) - pair
            weights = weight_ref[t]
            spread = jnp.zeros((pairs, 2 * tile), F32)
            for i in range(2):
                for j in range(2):
                    k = 4 * i + 2 * j
                    row = jnp.concatenate([weights[k : k + 1], weights[k + 1 : k + 2]], axis=1)
                    spread = jnp.where(at_pair == i * width_y + j, row, spread)
            total = (found.reshape(nvar, pairs, 2 * tile) * spread[None]).sum(axis=1)
            out_ref[t] = total[:, :tile] + total[:, tile:]

        @pl.when(live_ref[t] <= 0)
        def _():
            out_ref[t] = jnp.zeros((nvar, tile), F32)

        return carry

    lax.fori_loop(0, tiles, one, 0)


def gather(live, state, base, weights):
    nvar, rows, width_y, width_z = state.shape
    pairs = rows * width_y
    tiles, _, tile = base.shape
    vmem = pl.BlockSpec(memory_space=pltpu.VMEM)
    return pl.pallas_call(
        functools.partial(gather_kernel, (width_y, width_z.bit_length() - 1)),
        out_shape=jax.ShapeDtypeStruct((tiles, nvar, tile), F32),
        in_specs=[pl.BlockSpec(memory_space=pltpu.SMEM)] + [vmem] * 3,
        out_specs=vmem,
        scratch_shapes=[pltpu.VMEM((nvar * pairs, 2 * width_z), BF16)],
        compiler_params=pltpu.CompilerParams(vmem_limit_bytes=VMEM_LIMIT),
        name="gather",
    )(live, state.reshape(nvar, pairs, width_z), base, weights)


def scatter_kernel(
    comps, shift, state_ref, cell_ref, value_ref, out_ref,
    rows_ref, total, landing, send_sem, recv_sem,
):
    nvar, pairs, width_z = state_ref.shape
    slots, tile = cell_ref.shape[1], cell_ref.shape[3]
    barrier = pltpu.get_barrier_semaphore()
    greet_comps(comps, barrier)
    mine, copy = comp_copies(comps, value_ref, landing, send_sem, recv_sem)
    pl.semaphore_wait(barrier, comps - 1)
    for d in range(1, comps):
        copy(d).start()
    landing[0] = value_ref[mine]
    for s in range(slots):
        low_at = slice((2 * s + 1) * tile, (2 * s + 2) * tile)
        rows_ref[nvar * pairs :, low_at] = jnp.zeros((pairs, tile), BF16)

    def one(d, carry):
        @pl.when(d > 0)
        def _():
            copy(d).wait_recv()

        source = lax.rem(mine - d + comps, comps)
        hots = []
        for s in range(slots):
            cell = cell_ref[source, s]
            pair = lax.shift_right_arithmetic(cell, shift)
            depth = jnp.bitwise_and(cell, width_z - 1)
            hot = lax.broadcasted_iota(jnp.int32, (width_z, tile), 0) == depth
            hot = jnp.where(hot, 1.0, 0.0).astype(BF16)
            hots += [hot, hot]
            here = lax.broadcasted_iota(jnp.int32, (pairs, tile), 0) == pair
            values = landing[d, s]
            high = values.astype(BF16).astype(F32)
            low = values - high
            high_at = slice(2 * s * tile, (2 * s + 1) * tile)
            low_at = slice((2 * s + 1) * tile, (2 * s + 2) * tile)
            for v in range(nvar):
                at = slice(v * pairs, (v + 1) * pairs)
                rows_ref[at, high_at] = jnp.where(here, high[v : v + 1], 0.0).astype(BF16)
                rows_ref[at, low_at] = jnp.where(here, low[v : v + 1], 0.0).astype(BF16)
            rows_ref[nvar * pairs :, high_at] = jnp.where(here, 1.0, 0.0).astype(BF16)
        part = lax.dot_general(
            rows_ref[...], jnp.concatenate(hots, axis=1), (((1,), (1,)), ((), ())),
            preferred_element_type=F32,
        )

        @pl.when(d == 0)
        def _():
            total[...] = part

        @pl.when(d > 0)
        def _():
            total[...] += part

        return carry

    lax.fori_loop(0, comps, one, 0)
    hit = total[nvar * pairs :, :] > 0.5
    for v in range(nvar):
        out_ref[v] = jnp.where(hit, total[v * pairs : (v + 1) * pairs, :], state_ref[v])
    for d in range(1, comps):
        copy(d).wait_send()


def scatter(state, cells, values):
    nvar, rows, width_y, width_z = state.shape
    pairs = rows * width_y
    comps, slots, _, tile = cells.shape
    vmem = pl.BlockSpec(memory_space=pltpu.VMEM)
    out = pl.pallas_call(
        functools.partial(scatter_kernel, comps, width_z.bit_length() - 1),
        out_shape=jax.ShapeDtypeStruct((nvar, pairs, width_z), F32),
        in_specs=[vmem] * 3,
        out_specs=vmem,
        scratch_shapes=[
            pltpu.VMEM(((nvar + 1) * pairs, 2 * slots * tile), BF16),
            pltpu.VMEM(((nvar + 1) * pairs, width_z), F32),
            pltpu.VMEM(values.shape, F32),
            pltpu.SemaphoreType.DMA((comps,)),
            pltpu.SemaphoreType.DMA((comps,)),
        ],
        compiler_params=pltpu.CompilerParams(
            collective_id=2, has_side_effects=True, vmem_limit_bytes=VMEM_LIMIT
        ),
        name="scatter",
    )(state.reshape(nvar, pairs, width_z), cells, values)
    return out.reshape(state.shape)


def shards(
    state_now, state_prev, viscosity, jacobian, donor_cell, interp_weight, recv_cell, pair_tiles
):
    now = state_now[0]
    prev = state_prev[0]
    kappa = viscosity[0]
    jac = jacobian[0]
    nvar = now.shape[0]
    comps = lax.axis_size("comp")
    mine = lax.axis_index("comp")
    slots, corners, tile = donor_cell.shape[3:]
    tiles = comps * slots
    slot = jnp.arange(slots, dtype=jnp.int32)[None, :]
    live_in = lax.dynamic_index_in_dim(pair_tiles[0], mine, 1, keepdims=False)
    live_out = lax.dynamic_index_in_dim(pair_tiles[0], mine, 0, keepdims=False)
    keep = (slot < live_in[:, None]).reshape(comps, slots, 1, 1)
    cells = jnp.where(keep, recv_cell[0, 0].reshape(comps, slots, 1, tile), -1)
    send = (slot < live_out[:, None]).astype(jnp.int32).reshape(tiles)
    base = donor_cell[0, 0].reshape(tiles, corners, tile)[:, :1]
    state, held = relax(jac, now, now, prev, kappa, interp_weight[0, 0])
    held = held.reshape(tiles, corners, tile)
    for sub in range(SUBITERS):
        if sub > 0:
            (state,) = relax(jac, state, now, prev, kappa)
        packed = gather(send, state, base, held)
        state = scatter(state, cells, packed.reshape(comps, slots, nvar, tile))
    return state[None]


def solution(mesh):
    in_specs = (
        P("comp", None, "blk", None, None),
        P("comp", None, "blk", None, None),
        P("comp", "blk", None, None),
        P("comp", None, None, None),
        P("comp", "blk", None, None, None, None),
        P("comp", "blk", None, None, None, None),
        P("comp", "blk", None, None, None),
        P("blk", None, None),
    )
    out_specs = P("comp", None, "blk", None, None)
    return jax.shard_map(shards, mesh=mesh, in_specs=in_specs, out_specs=out_specs, check_vma=False)
```

profile of v0, /device:TPU:2, one launch (start us, length us, event | category | flops | bytes accessed | tf_op | source)
XLA Modules:
  0.0 122.8 jit_solution(11536084351225586856)
XLA Ops:
  0.0 0.0 copy-start
  0.0 0.7 copy-done
  0.7 0.2 dynamic-slice_reduce_fusion
  0.9 0.1 iota_compare_fusion.1
  1.0 0.1 fusion
  1.0 0.6 reshape.76.live_ref
  1.6 1.4 %broadcast_select_fusion.cell_ref = s32[8,2,1,128]{3,2,1,0:T(1,128)} fusion(s32[8,2,1,128]{3,2,1,0:T(1,128)} %bitcast.38, pred[8,2]{1,0:T(8,128)(4,1)S(1)} %iota_compare_fusion.1), kind=kLoop, calls=%fused_computation | loop fusion | flops 2048 | bytes 16400 | tf_op jit(solution)/shard_map/jit(_where)/select_n | solution.py:413
  3.0 1.4 %slice.4.base_ref = s32[16,1,128]{2,1,0:T(1,128)} slice(s32[16,8,128]{2,1,0:T(8,128)} %bitcast.39), slice={[0:16], [0:1], [0:128]} | slice | bytes 16384 | tf_op jit(solution)/shard_map/slice | solution.py:415
  4.4 1.3 %copy.11 = f32[1,3,6,6]{3,2,0,1:T(8,128)} copy(f32[1,3,6,6]{3,0,2,1:T(1,128)} %param.11) | data formatting | bytes 864
  5.7 35.9 %relax.2 = (f32[6,8,32,256]{3,2,1,0:T(8,128)}, f32[8,2,8,128]{3,2,1,0:T(8,128)}) custom-call(f32[3,6,6]{2,1,0:T(8,128)} %bitcast.35, f32[6,8,32,256]{3,2,1,0:T(8,128)} %bitcast.20, f32[6,8,32,256]{3,2,1,0:T(8,128)} %bitcast.21, f32[6,8,32,256]{3,2,1,0:T(8,128)} %bitcast.27, f32[8,32,256]{2,1,0:T(8,128)} %bitcast.29, f32[8,2,8,128]{3,2,1,0:T(8,128)} %bitcast.37), custom_call_target="tpu_custom_call" | custom-call | tf_op jit(solution)/shard_map/relax/pallas_call | solution.py:237
  41.7 8.4 %gather.2 = f32[16,6,128]{2,1,0:T(8,128)} custom-call(s32[16]{0:T(128)} %reshape.76.live_ref, f32[6,256,256]{2,1,0:T(8,128)} %bitcast.23, s32[16,1,128]{2,1,0:T(1,128)} %slice.4.base_ref, f32[16,8,128]{2,1,0:T(8,128)} %bitcast.31), custom_call_target="tpu_custom_call" | custom-call | tf_op jit(solution)/shard_map/gather/pallas_call | solution.py:296
  50.1 14.1 %scatter.2 = f32[6,256,256]{2,1,0:T(8,128)} custom-call(f32[6,256,256]{2,1,0:T(8,128)} %bitcast.24, s32[8,2,1,128]{3,2,1,0:T(1,128)} %broadcast_select_fusion.cell_ref, f32[8,2,6,128]{3,2,1,0:T(8,128)} %bitcast.34), custom_call_target="tpu_custom_call" | custom-call | tf_op jit(solution)/shard_map/scatter/pallas_call | solution.py:377
  64.2 33.4 %relax.3 = f32[6,8,32,256]{3,2,1,0:T(8,128)} custom-call(f32[3,6,6]{2,1,0:T(8,128)} %bitcast.36, f32[6,8,32,256]{3,2,1,0:T(8,128)} %bitcast.26, f32[6,8,32,256]{3,2,1,0:T(8,128)} %bitcast.22, f32[6,8,32,256]{3,2,1,0:T(8,128)} %bitcast.28, f32[8,32,256]{2,1,0:T(8,128)} %bitcast.30), custom_call_target="tpu_custom_call" | custom-call | tf_op jit(solution)/shard_map/relax/pallas_call | solution.py:237
  97.5 8.4 %gather.3 = f32[16,6,128]{2,1,0:T(8,128)} custom-call(s32[16]{0:T(128)} %reshape.76.live_ref, f32[6,256,256]{2,1,0:T(8,128)} %bitcast.18, s32[16,1,128]{2,1,0:T(1,128)} %slice.4.base_ref, f32[16,8,128]{2,1,0:T(8,128)} %bitcast.32), custom_call_target="tpu_custom_call" | custom-call | tf_op jit(solution)/shard_map/gather/pallas_call | solution.py:296
  105.9 14.1 %scatter.3 = f32[6,256,256]{2,1,0:T(8,128)} custom-call(f32[6,256,256]{2,1,0:T(8,128)} %bitcast.19, s32[8,2,1,128]{3,2,1,0:T(1,128)} %broadcast_select_fusion.cell_ref, f32[8,2,6,128]{3,2,1,0:T(8,128)} %bitcast.33), custom_call_target="tpu_custom_call" | custom-call | tf_op jit(solution)/shard_map/scatter/pallas_call | solution.py:377
  120.0 2.7 %copy.13 = f32[1,6,8,32,256]{4,3,2,1,0:T(8,128)} copy(f32[1,6,8,32,256]{4,3,2,1,0:T(8,128)} %bitcast.25) | data formatting | bytes 3145728
  (1 shorter events, 0.0 us)
Async XLA Ops:
  0.0 0.7 copy-start
where the time goes:
time: 125 us; the launch traced here: 123 us
  Pallas kernels  114 us (91%)
  local copies, waits for them, and re-layouts  6.93 us (6%)
  other arithmetic  1.51 us (1%)
    pallas_call x2, Pallas kernels, relax(): pl.pallas_call(functools.partial(relax_kernel, count, comps), out_shape=o...  69.3 us
    pallas_call x2, Pallas kernels, scatter(): pl.pallas_call(functools.partial(scatter_kernel, comps, width_z.bit_lengt...  28.2 us
    pallas_call x2, Pallas kernels, gather(): pl.pallas_call(functools.partial(gather_kernel, (width_y, width_z.bit_len...  16.8 us
    unnamed x4, local copies, waits for them, and re-layouts  4.71 us

commit v1 on v0

v1 whole, which is shorter than its diff:
```python
import functools

import jax
import jax.numpy as jnp
from jax import lax
from jax.experimental import pallas as pl
from jax.experimental.pallas import tpu as pltpu
from jax.sharding import PartitionSpec as P

SUBITERS = 2


time_scale = 0.5
pseudo_diag = 2.5

MESH = pl.DeviceIdType.MESH
VMEM_LIMIT = 60 * 1024 * 1024
F32 = jnp.float32
BF16 = jnp.bfloat16
I32 = jnp.int32
LANES = 128
SUB = 8
PAD = SUB


def split(value):
    high = value.astype(BF16)
    low = (value - high.astype(F32)).astype(BF16)
    return high, low


def flux_tile(src, coef, x, y, kappa, centred):
    nvar, _, halves, _, _ = src.shape
    lane = lax.broadcasted_iota(I32, (SUB, LANES), 1)
    total = [[None] * halves for _ in range(nvar)]
    for w in range(nvar):
        centre = [src[w, x + 1, h, pl.ds(PAD + y, SUB), :] for h in range(halves)]
        fore = [pltpu.roll(c, LANES - 1, 1) for c in centre]
        back = [pltpu.roll(c, 1, 1) for c in centre]
        for h in range(halves):
            next_z = jnp.where(lane == LANES - 1, fore[h + 1] if h + 1 < halves else 0.0, fore[h])
            last_z = jnp.where(lane == 0, back[h - 1] if h > 0 else 0.0, back[h])
            next_x = src[w, x + 2, h, pl.ds(PAD + y, SUB), :]
            last_x = src[w, x, h, pl.ds(PAD + y, SUB), :]
            next_y = src[w, x + 1, h, pl.ds(PAD + y + 1, SUB), :]
            last_y = src[w, x + 1, h, pl.ds(PAD + y - 1, SUB), :]
            beside = (next_x + last_x) + (next_y + last_y) + (next_z + last_z)
            if centred:
                own = kappa[h] * (6.0 * centre[h] - beside)
            else:
                own = -kappa[h] * beside
            total[w][h] = own if total[w][h] is None else total[w][h] + own
            diffs = (next_x - last_x, next_y - last_y, next_z - last_z)
            for v in range(nvar):
                term = None
                for d in range(3):
                    part = coef[(d * nvar + v) * nvar + w] * diffs[d]
                    term = part if term is None else term + part
                total[v][h] = term if total[v][h] is None else total[v][h] + term
    return total


def fill_hots(cells, row_hot, z_hot, shift):
    tiles, tile = cells.shape
    pairs = row_hot.shape[0]
    width_z = z_hot.shape[0]

    def one(t, carry):
        cell = cells[pl.ds(t, 1), :]
        pair = lax.shift_right_arithmetic(cell, shift)
        depth = jnp.bitwise_and(cell, width_z - 1)
        at = pl.ds(pl.multiple_of(t * tile, tile), tile)
        here = lax.broadcasted_iota(I32, (pairs, tile), 0) == pair
        row_hot[:, at] = jnp.where(here, 1.0, 0.0).astype(BF16)
        deep = lax.broadcasted_iota(I32, (width_z, tile), 0) == depth
        z_hot[:, at] = jnp.where(deep, 1.0, 0.0).astype(BF16)
        return carry

    lax.fori_loop(0, tiles, one, 0)


def fill_values(values, spread):
    comps, slots, nvar, tile = values.shape
    depth = spread.shape[1]

    def one(t, carry):
        high, low = split(values[lax.div(t, slots), lax.rem(t, slots)])
        at = pl.ds(pl.multiple_of(t * tile, tile), tile)
        for v in range(nvar):
            spread[v, :, at] = jnp.broadcast_to(high[v : v + 1].astype(F32), (depth, tile)).astype(BF16)
            spread[nvar + v, :, at] = jnp.broadcast_to(low[v : v + 1].astype(F32), (depth, tile)).astype(BF16)
        return carry

    lax.fori_loop(0, comps * slots, one, 0)


def place_plane(x, row_hot, z_hot, spread, placed):
    parts, depth, points = spread.shape
    width_y = placed.shape[0] // (parts + 1)

    def one(t, carry):
        at = pl.ds(pl.multiple_of(t * LANES, LANES), LANES)
        rows = row_hot[pl.ds(pl.multiple_of(x * width_y, width_y), width_y), at]
        for j in range(parts):
            value = jnp.concatenate([spread[j, :, at]] * (width_y // depth), axis=0)
            placed[j * width_y : (j + 1) * width_y, at] = rows * value
        placed[parts * width_y :, at] = rows
        return carry

    lax.fori_loop(0, points // LANES, one, 0)
    return lax.dot_general(placed[...], z_hot[...], (((1,), (1,)), ((), ())), preferred_element_type=F32)


def main_kernel(
    count, comps, jac_ref, live_ref, now_ref, prev_ref, kappa_ref, donor_ref, weight_ref, recv_ref,
    out_ref, arrived, cells,
    state, first, second, rstar, hist, kappa, scale, coef,
    packed, values, held, weight_land, landing, row_hot, z_hot, spread, placed,
    load_sem, halo_send, halo_recv, weight_send, weight_recv, value_send, value_recv, save_sem,
):
    me = lax.axis_index("blk")
    mine = lax.axis_index("comp")
    right = lax.rem(me + 1, count)
    left = lax.rem(me + count - 1, count)
    has_left = me > 0
    has_right = me < count - 1
    nvar, rows, halves, width_y, _ = rstar.shape
    width_z = halves * LANES
    shift = width_z.bit_length() - 1
    chunks = width_y // SUB
    slots, corners, tile = donor_ref.shape[1:]
    fields = [state, first, second]
    inside = pl.ds(PAD, width_y)
    edge = rows - 1

    def lanes(h):
        return pl.ds(h * LANES, LANES)

    loads = []
    for h in range(halves):
        for x in (0, edge):
            loads.append((now_ref.at[:, x, :, lanes(h)], state.at[:, x + 1, h, inside, :]))
    for h in range(halves):
        loads.append((now_ref.at[:, pl.ds(1, rows - 2), :, lanes(h)], state.at[:, pl.ds(2, rows - 2), h, inside, :]))
    for h in range(halves):
        loads.append((kappa_ref.at[:, :, lanes(h)], kappa.at[:, h]))
    for h in range(halves):
        loads.append((prev_ref.at[:, :, :, lanes(h)], hist.at[:, :, h]))
    loads = [pltpu.make_async_copy(src, dst, load_sem.at[i]) for i, (src, dst) in enumerate(loads)]
    for load in loads:
        load.start()

    barrier = pltpu.get_barrier_semaphore()

    @pl.when(has_left)
    def _():
        pl.semaphore_signal(barrier, inc=1, device_id={"blk": left}, device_id_type=MESH)

    @pl.when(has_right)
    def _():
        pl.semaphore_signal(barrier, inc=1, device_id={"blk": right}, device_id_type=MESH)

    for d in range(1, comps):
        peer = lax.rem(mine + d, comps)
        pl.semaphore_signal(barrier, inc=1, device_id={"comp": peer}, device_id_type=MESH)

    def blank_pads(x, carry):
        for field in fields:
            for v in range(nvar):
                for h in range(halves):
                    field[v, x + 1, h, 0:PAD, :] = jnp.zeros((PAD, LANES), F32)
                    field[v, x + 1, h, PAD + width_y :, :] = jnp.zeros((field.shape[3] - PAD - width_y, LANES), F32)
        return carry

    lax.fori_loop(0, rows, blank_pads, 0)

    def blank_plane(x):
        for field in fields:
            for v in range(nvar):
                for h in range(halves):
                    field[v, x, h, PAD : PAD + width_y, :] = jnp.zeros((width_y, LANES), F32)

    @pl.when(jnp.logical_not(has_left))
    def _():
        blank_plane(0)

    @pl.when(jnp.logical_not(has_right))
    def _():
        blank_plane(rows + 1)

    def to_left(sub, k, c):
        at = pl.ds(PAD + c * SUB, SUB)
        return pltpu.make_async_remote_copy(
            src_ref=fields[k].at[:, 1, :, at, :], dst_ref=fields[k].at[:, rows + 1, :, at, :],
            send_sem=halo_send.at[sub, k, 1, c], recv_sem=halo_recv.at[sub, k, 1, c],
            device_id={"blk": left}, device_id_type=MESH,
        )

    def to_right(sub, k, c):
        at = pl.ds(PAD + c * SUB, SUB)
        return pltpu.make_async_remote_copy(
            src_ref=fields[k].at[:, rows, :, at, :], dst_ref=fields[k].at[:, 0, :, at, :],
            send_sem=halo_send.at[sub, k, 0, c], recv_sem=halo_recv.at[sub, k, 0, c],
            device_id={"blk": right}, device_id_type=MESH,
        )

    def start(sub, k, c):
        @pl.when(has_left)
        def _():
            to_left(sub, k, c).start()

        @pl.when(has_right)
        def _():
            to_right(sub, k, c).start()

    def arrive(sub, k, c):
        @pl.when(has_left)
        def _():
            to_right(sub, k, c).wait_recv()

        @pl.when(has_right)
        def _():
            to_left(sub, k, c).wait_recv()

    def sent(sub, k):
        for c in range(chunks):
            @pl.when(has_left)
            def _(c=c):
                to_left(sub, k, c).wait_send()

            @pl.when(has_right)
            def _(c=c):
                to_right(sub, k, c).wait_send()

    def comp_copy(d, source, target, send_sem, recv_sem):
        peer = lax.rem(mine + d, comps)
        return pltpu.make_async_remote_copy(
            src_ref=source.at[peer], dst_ref=target.at[d], send_sem=send_sem, recv_sem=recv_sem,
            device_id={"comp": peer}, device_id_type=MESH,
        )

    def weight_copy(d):
        return comp_copy(d, weight_ref, weight_land, weight_send.at[d], weight_recv.at[d])

    def value_copy(sub, d):
        return comp_copy(d, values.at[sub], landing.at[sub], value_send.at[sub, d], value_recv.at[sub, d])

    def tile_step(k, x, c):
        y = c * SUB
        at = pl.ds(y, SUB)
        own = [kappa[x, h, at, :] for h in range(halves)]
        flow = flux_tile(fields[k], coef, x, y, own, k == 0)
        for h in range(halves):
            factor = scale[x, h, at, :]
            for v in range(nvar):
                centre = fields[0][v, x + 1, h, pl.ds(PAD + y, SUB), :]
                if k == 0:
                    base = (3.0 * time_scale) * centre + hist[v, x, h, at, :] + flow[v][h]
                    rstar[v, x, h, at, :] = base
                    first[v, x + 1, h, pl.ds(PAD + y, SUB), :] = base * factor
                else:
                    step = (rstar[v, x, h, at, :] + flow[v][h]) * factor
                    if k == 1:
                        second[v, x + 1, h, pl.ds(PAD + y, SUB), :] = step
                    else:
                        state[v, x + 1, h, pl.ds(PAD + y, SUB), :] = centre + step

    def planes(k, low, high):
        def one(x, carry):
            for c in range(chunks):
                tile_step(k, x, c)
            return carry

        lax.fori_loop(low, high, one, 0)

    def edges(k, c):
        def one(i, carry):
            tile_step(k, i * edge, c)
            return carry

        lax.fori_loop(0, 2, one, 0)

    def pack(low, high, stride, place):
        def one(i, carry):
            x = low + i * stride
            for v in range(nvar):
                at = pl.ds(pl.multiple_of(((place + i) * nvar + v) * width_y, width_y), width_y)
                for h in range(halves):
                    upper, lower = split(state[v, x + 1, h, inside, :])
                    packed[at, h * LANES : (h + 1) * LANES] = upper
                    packed[at, width_z + h * LANES : width_z + (h + 1) * LANES] = lower
            return carry

        lax.fori_loop(0, high, one, 0)

    def interpolate(target, c, s, where, place):
        base = donor_ref[c, s, 0:1, :]
        weights = held[c, s]
        pair = lax.shift_right_logical(base, shift)
        depth = jnp.bitwise_and(base, width_z - 1)
        depth = jnp.concatenate([depth, depth + 1], axis=1)
        pair = jnp.concatenate([pair, pair], axis=1)
        at_z = lax.broadcasted_iota(I32, (width_z, 2 * tile), 0)
        hot = jnp.where(at_z == depth, 1.0, 0.0).astype(BF16)
        hot = jnp.concatenate([hot, hot], axis=0)
        size = nvar * width_y
        found = jnp.dot(packed[place * size : (place + len(where)) * size, :], hot, preferred_element_type=F32)
        total = None
        for i, x in enumerate(where):
            at_pair = lax.broadcasted_iota(I32, (width_y, 2 * tile), 0) + x * width_y - pair
            spread_row = jnp.zeros((width_y, 2 * tile), F32)
            for a in range(2):
                for b in range(2):
                    k = 4 * a + 2 * b
                    row = jnp.concatenate([weights[k : k + 1], weights[k + 1 : k + 2]], axis=1)
                    spread_row = jnp.where(at_pair == a * width_y + b, row, spread_row)
            part = found[i * size : (i + 1) * size].reshape(nvar, width_y, 2 * tile) * spread_row[None]
            total = part if total is None else total + part
        total = total.sum(axis=1)
        return total[:, :tile] + total[:, tile:]

    for load in loads[: 2 * halves]:
        load.wait()
    blocks = has_left.astype(I32) + has_right.astype(I32)
    pl.semaphore_wait(barrier, blocks + comps - 1)
    for c in range(chunks):
        start(0, 0, c)
    for d in range(1, comps):
        weight_copy(d).start()
    for d in range(3):
        for v in range(nvar):
            for w in range(nvar):
                coef[(d * nvar + v) * nvar + w] = jnp.full((SUB, LANES), 0.5 * jac_ref[d, v, w], F32)
    for load in loads[2 * halves :]:
        load.wait()

    def prepare(x, carry):
        scale[x] = -1.0 / (pseudo_diag + 6.0 * kappa[x])
        for v in range(nvar):
            hist[v, x] = time_scale * hist[v, x] - (4.0 * time_scale) * state[v, x + 1, :, inside, :]
        return carry

    lax.fori_loop(0, rows, prepare, 0)

    for sub in range(SUBITERS):
        planes(0, 1, edge)
        if sub == 0:
            for c in range(comps):
                alive = live_ref[c, mine]
                slot = lax.broadcasted_iota(I32, (slots, tile), 0)
                cells[c * slots : (c + 1) * slots, :] = jnp.where(slot < alive, recv_ref[c], -1)
            fill_hots(cells, row_hot, z_hot, shift)
        for c in range(chunks):
            arrive(sub, 0, c)
            edges(0, c)
            start(sub, 1, c)
        low = 1
        for c in range(chunks):
            arrive(sub, 1, c)
            edges(1, c)
            start(sub, 2, c)
            high = low + (edge - low + chunks - c - 1) // (chunks - c)
            planes(1, low, high)
            low = high
        if sub == 0:
            for d in range(1, comps):
                weight_copy(d).wait()
                held[lax.rem(mine - d + comps, comps)] = weight_land[d]
            held[mine] = weight_ref[mine]
        planes(2, 1, edge)
        pack(1, rows - 2, 1, 0)

        def interior(c, carry, sub=sub):
            for s in range(slots):
                values[sub, c, s] = interpolate(sub, c, s, tuple(range(1, edge)), 0)
            return carry

        lax.fori_loop(0, comps, interior, 0)
        sent(sub, 0)
        for c in range(chunks):
            arrive(sub, 2, c)
            edges(2, c)
        pack(0, 2, edge, rows - 2)

        def boundary(d, carry, sub=sub):
            peer = lax.rem(mine + d, comps)
            for s in range(slots):
                values[sub, peer, s] += interpolate(sub, peer, s, (0, edge), rows - 2)

            @pl.when(d > 1)
            def _():
                value_copy(sub, d - 1).start()

            return carry

        lax.fori_loop(1, comps + 1, boundary, 0)
        if sub == SUBITERS - 1:
            saves = [
                pltpu.make_async_copy(
                    state.at[:, pl.ds(1, rows), h, inside, :], out_ref.at[:, :, :, lanes(h)], save_sem.at[h]
                )
                for h in range(halves)
            ]
            for save in saves:
                save.start()
        sent(sub, 1)
        sent(sub, 2)
        arrived[mine] = values[sub, mine]

        def collect(d, carry, sub=sub):
            value_copy(sub, d).wait_recv()
            arrived[lax.rem(mine - d + comps, comps)] = landing[sub, d]
            return carry

        lax.fori_loop(1, comps, collect, 0)
        if sub < SUBITERS - 1:
            fill_values(arrived, spread)

            def place(x):
                part = place_plane(x, row_hot, z_hot, spread, placed)
                hit = part[2 * nvar * width_y :, :] > 0.5
                for v in range(nvar):
                    value = part[v * width_y : (v + 1) * width_y] + part[(nvar + v) * width_y : (nvar + v + 1) * width_y]
                    for h in range(halves):
                        side = slice(h * LANES, (h + 1) * LANES)
                        old = state[v, x + 1, h, inside, :]
                        state[v, x + 1, h, inside, :] = jnp.where(hit[:, side], value[:, side], old)

            def outer(i, carry):
                place(i * edge)
                return carry

            lax.fori_loop(0, 2, outer, 0)
            for c in range(chunks):
                start(sub + 1, 0, c)

            def inner(x, carry):
                place(x)
                return carry

            lax.fori_loop(1, edge, inner, 0)
    for sub in range(SUBITERS):
        for d in range(1, comps):
            value_copy(sub, d).wait_send()
    for save in saves:
        save.wait()


def run_main(jac, live, now, prev, kappa, donor, weights, recv):
    count = lax.axis_size("blk")
    nvar, rows, width_y, width_z = now.shape
    comps, slots, corners, tile = weights.shape
    halves = width_z // LANES
    chunks = width_y // SUB
    points = comps * slots * tile
    pairs = rows * width_y
    vmem = pl.BlockSpec(memory_space=pltpu.VMEM)
    smem = pl.BlockSpec(memory_space=pltpu.SMEM)
    hbm = pl.BlockSpec(memory_space=pl.ANY)
    field = pltpu.VMEM((nvar, rows + 2, halves, width_y + 2 * PAD, LANES), F32)
    plain = pltpu.VMEM((nvar, rows, halves, width_y, LANES), F32)
    single = pltpu.VMEM((rows, halves, width_y, LANES), F32)
    dma = pltpu.SemaphoreType.DMA
    fringe = (comps, slots, nvar, tile)
    scratch = [
        field, field, field, plain, plain, single, single,
        pltpu.VMEM((3 * nvar * nvar, SUB, LANES), F32),
        pltpu.VMEM((nvar * pairs, 2 * width_z), BF16),
        pltpu.VMEM((SUBITERS,) + fringe, F32),
        pltpu.VMEM(weights.shape, F32),
        pltpu.VMEM(weights.shape, F32),
        pltpu.VMEM((SUBITERS,) + fringe, F32),
        pltpu.VMEM((pairs, points), BF16),
        pltpu.VMEM((width_z, points), BF16),
        pltpu.VMEM((2 * nvar, 2 * SUB, points), BF16),
        pltpu.VMEM(((2 * nvar + 1) * width_y, points), BF16),
        dma((6 * halves,)),
        dma((SUBITERS, 3, 2, chunks)), dma((SUBITERS, 3, 2, chunks)),
        dma((comps,)), dma((comps,)),
        dma((SUBITERS, comps)), dma((SUBITERS, comps)),
        dma((halves,)),
    ]
    return pl.pallas_call(
        functools.partial(main_kernel, count, comps),
        out_shape=[
            jax.ShapeDtypeStruct(now.shape, F32),
            jax.ShapeDtypeStruct(fringe, F32),
            jax.ShapeDtypeStruct((comps * slots, tile), I32),
        ],
        in_specs=[smem, smem, hbm, hbm, hbm, vmem, vmem, vmem],
        out_specs=[hbm, vmem, vmem],
        scratch_shapes=scratch,
        compiler_params=pltpu.CompilerParams(
            collective_id=0, has_side_effects=True, vmem_limit_bytes=VMEM_LIMIT
        ),
        name="subiterate",
    )(jac, live, now, prev, kappa, donor, weights, recv)


def finish_kernel(shift, state_ref, cells_ref, value_ref, out_ref, row_hot, z_hot, spread, placed):
    nvar, _, width_y, width_z = state_ref.shape
    x = pl.program_id(0)

    @pl.when(x == 0)
    def _():
        fill_hots(cells_ref, row_hot, z_hot, shift)
        fill_values(value_ref, spread)

    part = place_plane(x, row_hot, z_hot, spread, placed)
    hit = part[2 * nvar * width_y :, :] > 0.5
    for v in range(nvar):
        value = part[v * width_y : (v + 1) * width_y] + part[(nvar + v) * width_y : (nvar + v + 1) * width_y]
        out_ref[v, 0] = jnp.where(hit, value, state_ref[v, 0])


def run_finish(state, cells, values):
    nvar, rows, width_y, width_z = state.shape
    points = cells.shape[0] * cells.shape[1]
    block = pl.BlockSpec((nvar, 1, width_y, width_z), lambda x: (0, x, 0, 0))
    vmem = pl.BlockSpec(memory_space=pltpu.VMEM)
    return pl.pallas_call(
        functools.partial(finish_kernel, width_z.bit_length() - 1),
        grid=(rows,),
        out_shape=jax.ShapeDtypeStruct(state.shape, F32),
        in_specs=[block, vmem, vmem],
        out_specs=block,
        scratch_shapes=[
            pltpu.VMEM((rows * width_y, points), BF16),
            pltpu.VMEM((width_z, points), BF16),
            pltpu.VMEM((2 * nvar, 2 * SUB, points), BF16),
            pltpu.VMEM(((2 * nvar + 1) * width_y, points), BF16),
        ],
        compiler_params=pltpu.CompilerParams(vmem_limit_bytes=VMEM_LIMIT),
        name="finish",
    )(state, cells, values)


def shards(
    state_now, state_prev, viscosity, jacobian, donor_cell, interp_weight, recv_cell, pair_tiles
):
    state, values, cells = run_main(
        jacobian[0], pair_tiles[0], state_now[0], state_prev[0], viscosity[0],
        donor_cell[0, 0], interp_weight[0, 0], recv_cell[0, 0],
    )
    return run_finish(state, cells, values)[None]


def solution(mesh):
    in_specs = (
        P("comp", None, "blk", None, None),
        P("comp", None, "blk", None, None),
        P("comp", "blk", None, None),
        P("comp", None, None, None),
        P("comp", "blk", None, None, None, None),
        P("comp", "blk", None, None, None, None),
        P("comp", "blk", None, None, None),
        P("blk", None, None),
    )
    out_specs = P("comp", None, "blk", None, None)
    return jax.shard_map(shards, mesh=mesh, in_specs=in_specs, out_specs=out_specs, check_vma=False)
```

time: 125 us -> 97.3 us (0.78); the launches traced: 123 us -> 96.6 us
  Pallas kernels: 114 us -> 95.3 us
  local copies, waits for them, and re-layouts: 6.93 us -> 1.3 us
  other arithmetic: 1.51 us -> 0 us
    pallas_call x6 -> x2, Pallas kernels: 114 us -> 95.3 us  [the longest x1 82.5 us: run_main(): pl.pallas_call(functools.partial(main_kernel, count, comps), out_shape=[j...]
    unnamed x4 -> x1, local copies, waits for them, and re-layouts: 4.71 us -> 1.3 us
    slice x1 -> x0, local copies, waits for them, and re-layouts: 1.43 us -> none  [shards(): base = donor_cell[0, 0].reshape(tiles, corners, tile)[:, :1]]
    select_n x1 -> x0, other arithmetic: 1.36 us -> none  [shards(): cells = jnp.where(keep, recv_cell[0, 0].reshape(comps, slots, 1, tile), -1)]
where the time goes in v1:
time: 97.3 us; the launch traced here: 96.6 us
  Pallas kernels  95.3 us (98%)
  local copies, waits for them, and re-layouts  1.3 us (1%)
    pallas_call x1, Pallas kernels, run_main(): pl.pallas_call(functools.partial(main_kernel, count, comps), out_shape=[j...  82.5 us
    pallas_call x1, Pallas kernels, run_finish(): pl.pallas_call(functools.partial(finish_kernel, width_z.bit_length() - 1)...  12.7 us

profile of v1, /device:TPU:2, one launch (start us, length us, event | category | flops | bytes accessed | tf_op | source)
XLA Modules:
  0.0 96.6 jit_solution(7860798458279790903)
XLA Ops:
  0.0 1.3 %copy.11 = f32[1,3,6,6]{3,2,0,1:T(8,128)} copy(f32[1,3,6,6]{3,0,2,1:T(1,128)} %param.11) | data formatting | bytes 864
  1.3 82.5 %subiterate.1 = (f32[6,8,32,256]{3,2,1,0:T(8,128)}, f32[8,2,6,128]{3,2,1,0:T(8,128)}, s32[16,128]{1,0:T(8,128)}) custom-call(f32[3,6,6]{2,1,0:T(8,128)} %bitcast.16, s32[8,8]{1,0:T(8,128)} %bitcast.18, f32[6,8,32,256]{3,2,1,0:T(8,128)} %bitcast.11, f32[6,8,32,256]{3,2,1,0:T(8,128)} %bitcast.12, f32[8,32,256]{2,1,0:T(8,128)} %bitcast.13, ...), custom_call_target="tpu_custom_call" | custom-call | tf_op jit(solution)/shard_map/subiterate/pallas_call | solution.py:483
  83.8 12.7 %finish.1 = f32[6,8,32,256]{3,2,1,0:T(8,128)} custom-call(f32[6,8,32,256]{3,2,1,0:T(8,128)} %get-tuple-element.8.state_ref, s32[16,128]{1,0:T(8,128)} %get-tuple-element.9.cells_ref, f32[8,2,6,128]{3,2,1,0:T(8,128)} %get-tuple-element.10.value_ref), custom_call_target="tpu_custom_call" | custom-call | tf_op jit(solution)/shard_map/finish/pallas_call | solution.py:521

commit v2 on v1

--- a/solution.py
+++ b/solution.py
@@ -94,29 +94,36 @@
     lax.fori_loop(0, comps * slots, one, 0)
 
 
-def place_plane(x, row_hot, z_hot, spread, placed):
+def place_planes(planes, width_y, row_hot, z_hot, spread):
     parts, depth, points = spread.shape
-    width_y = placed.shape[0] // (parts + 1)
-
-    def one(t, carry):
-        at = pl.ds(pl.multiple_of(t * LANES, LANES), LANES)
-        rows = row_hot[pl.ds(pl.multiple_of(x * width_y, width_y), width_y), at]
-        for j in range(parts):
-            value = jnp.concatenate([spread[j, :, at]] * (width_y // depth), axis=0)
-            placed[j * width_y : (j + 1) * width_y, at] = rows * value
-        placed[parts * width_y :, at] = rows
-        return carry
-
-    lax.fori_loop(0, points // LANES, one, 0)
-    return lax.dot_general(placed[...], z_hot[...], (((1,), (1,)), ((), ())), preferred_element_type=F32)
+    nvar = parts // 2
+    chunk = 2 * LANES
+    total = None
+    for t in range(points // chunk):
+        at = pl.ds(t * chunk, chunk)
+        blocks = []
+        for x in planes:
+            rows = row_hot[pl.ds(pl.multiple_of(x * width_y, width_y), width_y), at]
+            for j in range(parts):
+                blocks.append(rows * jnp.concatenate([spread[j, :, at]] * (width_y // depth), axis=0))
+            blocks.append(rows)
+        part = lax.dot_general(
+            jnp.concatenate(blocks, axis=0), z_hot[:, at], (((1,), (1,)), ((), ())), preferred_element_type=F32
+        )
+        total = part if total is None else total + part
+    results = []
+    for i in range(len(planes)):
+        rows = [total[(i * (parts + 1) + j) * width_y :][:width_y] for j in range(parts + 1)]
+        results.append(([rows[v] + rows[nvar + v] for v in range(nvar)], rows[parts] > 0.5))
+    return results
 
 
 def main_kernel(
     count, comps, jac_ref, live_ref, now_ref, prev_ref, kappa_ref, donor_ref, weight_ref, recv_ref,
     out_ref, arrived, cells,
     state, first, second, rstar, hist, kappa, scale, coef,
-    packed, values, held, weight_land, landing, row_hot, z_hot, spread, placed,
-    load_sem, halo_send, halo_recv, weight_send, weight_recv, value_send, value_recv, save_sem,
+    packed, values, held, weight_land, landing, row_hot, z_hot, spread, z_pick, row_weight, inner_part, passing,
+    load_sem, halo_send, halo_recv, pass_send, pass_recv, weight_send, weight_recv, value_send, value_recv, save_sem,
 ):
     me = lax.axis_index("blk")
     mine = lax.axis_index("comp")
@@ -132,6 +139,7 @@
     fields = [state, first, second]
     inside = pl.ds(PAD, width_y)
     edge = rows - 1
+    group = 2
 
     def lanes(h):
         return pl.ds(h * LANES, LANES)
@@ -164,6 +172,12 @@
         peer = lax.rem(mine + d, comps)
         pl.semaphore_signal(barrier, inc=1, device_id={"comp": peer}, device_id_type=MESH)
 
+    detour = chunks // 4 if count == 4 else 0
+    direct = chunks - detour
+    across = lax.rem(me + 2, count)
+    if detour:
+        pl.semaphore_signal(barrier, inc=1, device_id={"blk": across}, device_id_type=MESH)
+
     def blank_pads(x, carry):
         for field in fields:
             for v in range(nvar):
@@ -204,14 +218,69 @@
             device_id={"blk": right}, device_id_type=MESH,
         )
 
+    def aside(sub, k, c, x, side):
+        at = pl.ds(PAD + c * SUB, SUB)
+        return pltpu.make_async_remote_copy(
+            src_ref=fields[k].at[:, x, :, at, :], dst_ref=passing.at[sub, k, c - direct],
+            send_sem=halo_send.at[sub, k, side, c], recv_sem=pass_recv.at[sub, k, c - direct],
+            device_id={"blk": across}, device_id_type=MESH,
+        )
+
+    def onward(sub, k, c, x, side, target):
+        at = pl.ds(PAD + c * SUB, SUB)
+        return pltpu.make_async_remote_copy(
+            src_ref=passing.at[sub, k, c - direct], dst_ref=fields[k].at[:, x, :, at, :],
+            send_sem=pass_send.at[sub, k, c - direct], recv_sem=halo_recv.at[sub, k, side, c],
+            device_id={"blk": target}, device_id_type=MESH,
+        )
+
     def start(sub, k, c):
-        @pl.when(has_left)
-        def _():
-            to_left(sub, k, c).start()
-
-        @pl.when(has_right)
-        def _():
-            to_right(sub, k, c).start()
+        if c < direct:
+            @pl.when(has_left)
+            def _():
+                to_left(sub, k, c).start()
+
+            @pl.when(has_right)
+            def _():
+                to_right(sub, k, c).start()
+        else:
+            @pl.when(jnp.logical_or(me == 1, me == 3))
+            def _():
+                to_left(sub, k, c).start()
+
+            @pl.when(me == 2)
+            def _():
+                aside(sub, k, c, 1, 1).start()
+
+            @pl.when(jnp.logical_or(me == 0, me == 2))
+            def _():
+                to_right(sub, k, c).start()
+
+            @pl.when(me == 1)
+            def _():
+                aside(sub, k, c, rows, 0).start()
+
+    def forward(sub, k, c):
+        if c >= direct:
+            @pl.when(me == 3)
+            def _():
+                aside(sub, k, c, rows, 0).wait_recv()
+                onward(sub, k, c, 0, 0, left).start()
+
+            @pl.when(me == 0)
+            def _():
+                aside(sub, k, c, 1, 1).wait_recv()
+                onward(sub, k, c, rows + 1, 1, right).start()
+
+    def forwarded(sub, k):
+        for c in range(direct, chunks):
+            @pl.when(me == 3)
+            def _(c=c):
+                onward(sub, k, c, 0, 0, left).wait_send()
+
+            @pl.when(me == 0)
+            def _(c=c):
+                onward(sub, k, c, rows + 1, 1, right).wait_send()
 
     def arrive(sub, k, c):
         @pl.when(has_left)
@@ -293,7 +362,8 @@
 
         lax.fori_loop(0, high, one, 0)
 
-    def interpolate(target, c, s, where, place):
+    def fill_picks(t, carry):
+        c, s = lax.div(t, slots), lax.rem(t, slots)
         base = donor_ref[c, s, 0:1, :]
         weights = held[c, s]
         pair = lax.shift_right_logical(base, shift)
@@ -301,28 +371,32 @@
         depth = jnp.concatenate([depth, depth + 1], axis=1)
         pair = jnp.concatenate([pair, pair], axis=1)
         at_z = lax.broadcasted_iota(I32, (width_z, 2 * tile), 0)
-        hot = jnp.where(at_z == depth, 1.0, 0.0).astype(BF16)
-        hot = jnp.concatenate([hot, hot], axis=0)
+        z_pick[t] = jnp.where(at_z == depth, 1.0, 0.0).astype(BF16)
+        at_pair = lax.broadcasted_iota(I32, (rows * width_y, 2 * tile), 0) - pair
+        spread_row = jnp.zeros((rows * width_y, 2 * tile), F32)
+        for a in range(2):
+            for b in range(2):
+                k = 4 * a + 2 * b
+                row = jnp.concatenate([weights[k : k + 1], weights[k + 1 : k + 2]], axis=1)
+                spread_row = jnp.where(at_pair == a * width_y + b, row, spread_row)
+        row_weight[t] = spread_row
+        return carry
+
+    def interpolate(t, where, place):
         size = nvar * width_y
+        hot = jnp.concatenate([z_pick[t], z_pick[t]], axis=0)
         found = jnp.dot(packed[place * size : (place + len(where)) * size, :], hot, preferred_element_type=F32)
         total = None
         for i, x in enumerate(where):
-            at_pair = lax.broadcasted_iota(I32, (width_y, 2 * tile), 0) + x * width_y - pair
-            spread_row = jnp.zeros((width_y, 2 * tile), F32)
-            for a in range(2):
-                for b in range(2):
-                    k = 4 * a + 2 * b
-                    row = jnp.concatenate([weights[k : k + 1], weights[k + 1 : k + 2]], axis=1)
-                    spread_row = jnp.where(at_pair == a * width_y + b, row, spread_row)
-            part = found[i * size : (i + 1) * size].reshape(nvar, width_y, 2 * tile) * spread_row[None]
+            weight = row_weight[t, x * width_y : (x + 1) * width_y, :].reshape(1, chunks, SUB, 2 * tile)
+            part = (found[i * size : (i + 1) * size].reshape(nvar, chunks, SUB, 2 * tile) * weight).sum(axis=1)
             total = part if total is None else total + part
-        total = total.sum(axis=1)
-        return total[:, :tile] + total[:, tile:]
+        return total
 
     for load in loads[: 2 * halves]:
         load.wait()
     blocks = has_left.astype(I32) + has_right.astype(I32)
-    pl.semaphore_wait(barrier, blocks + comps - 1)
+    pl.semaphore_wait(barrier, blocks + comps - 1 + (1 if detour else 0))
     for c in range(chunks):
         start(0, 0, c)
     for d in range(1, comps):
@@ -343,57 +417,78 @@
     lax.fori_loop(0, rows, prepare, 0)
 
     for sub in range(SUBITERS):
-        planes(0, 1, edge)
+        if sub == 0:
+            planes(0, 1, edge)
+        for c in range(direct, chunks):
+            forward(sub, 0, c)
+        if sub > 0:
+            planes(0, 1, edge)
         if sub == 0:
             for c in range(comps):
                 alive = live_ref[c, mine]
                 slot = lax.broadcasted_iota(I32, (slots, tile), 0)
                 cells[c * slots : (c + 1) * slots, :] = jnp.where(slot < alive, recv_ref[c], -1)
             fill_hots(cells, row_hot, z_hot, shift)
+            for d in range(1, comps):
+                weight_copy(d).wait()
+                held[lax.rem(mine - d + comps, comps)] = weight_land[d]
+            held[mine] = weight_ref[mine]
+            lax.fori_loop(0, comps * slots, fill_picks, 0)
         for c in range(chunks):
             arrive(sub, 0, c)
             edges(0, c)
             start(sub, 1, c)
         low = 1
         for c in range(chunks):
+            if c + direct < chunks:
+                forward(sub, 1, c + direct)
             arrive(sub, 1, c)
             edges(1, c)
             start(sub, 2, c)
             high = low + (edge - low + chunks - c - 1) // (chunks - c)
             planes(1, low, high)
             low = high
-        if sub == 0:
-            for d in range(1, comps):
-                weight_copy(d).wait()
-                held[lax.rem(mine - d + comps, comps)] = weight_land[d]
-            held[mine] = weight_ref[mine]
-        planes(2, 1, edge)
+        half = (edge + 1) // 2
+        for c in range(direct, chunks - 1):
+            forward(sub, 2, c)
+        planes(2, 1, half)
+        if detour:
+            forward(sub, 2, chunks - 1)
+        planes(2, half, edge)
         pack(1, rows - 2, 1, 0)
 
-        def interior(c, carry, sub=sub):
-            for s in range(slots):
-                values[sub, c, s] = interpolate(sub, c, s, tuple(range(1, edge)), 0)
+        def interior(i, carry):
+            tiles = [i * group * slots + j for j in range(group * slots)]
+            found = [interpolate(t, tuple(range(1, edge)), 0) for t in tiles]
+            for t, part in zip(tiles, found):
+                inner_part[t] = part
             return carry
 
-        lax.fori_loop(0, comps, interior, 0)
+        lax.fori_loop(0, comps // group, interior, 0)
         sent(sub, 0)
         for c in range(chunks):
             arrive(sub, 2, c)
             edges(2, c)
         pack(0, 2, edge, rows - 2)
 
-        def boundary(d, carry, sub=sub):
-            peer = lax.rem(mine + d, comps)
-            for s in range(slots):
-                values[sub, peer, s] += interpolate(sub, peer, s, (0, edge), rows - 2)
-
-            @pl.when(d > 1)
-            def _():
-                value_copy(sub, d - 1).start()
+        def boundary(i, carry, sub=sub):
+            peers = [lax.rem(mine + i * group + 1 + j, comps) for j in range(group)]
+            tiles = [(peer, s) for peer in peers for s in range(slots)]
+            found = [interpolate(peer * slots + s, (0, edge), rows - 2) for peer, s in tiles]
+            for (peer, s), part in zip(tiles, found):
+                total = (part + inner_part[peer * slots + s]).sum(axis=1)
+                values[sub, peer, s] = total[:, :tile] + total[:, tile:]
+
+            @pl.when(i > 0)
+            def _():
+                for j in range(group):
+                    value_copy(sub, (i - 1) * group + 1 + j).start()
 
             return carry
 
-        lax.fori_loop(1, comps + 1, boundary, 0)
+        lax.fori_loop(0, comps // group, boundary, 0)
+        for d in range(comps - group + 1, comps):
+            value_copy(sub, d).start()
         if sub == SUBITERS - 1:
             saves = [
                 pltpu.make_async_copy(
@@ -405,6 +500,8 @@
                 save.start()
         sent(sub, 1)
         sent(sub, 2)
+        for k in range(3):
+            forwarded(sub, k)
         arrived[mine] = values[sub, mine]
 
         def collect(d, carry, sub=sub):
@@ -416,29 +513,23 @@
         if sub < SUBITERS - 1:
             fill_values(arrived, spread)
 
-            def place(x):
-                part = place_plane(x, row_hot, z_hot, spread, placed)
-                hit = part[2 * nvar * width_y :, :] > 0.5
-                for v in range(nvar):
-                    value = part[v * width_y : (v + 1) * width_y] + part[(nvar + v) * width_y : (nvar + v + 1) * width_y]
-                    for h in range(halves):
-                        side = slice(h * LANES, (h + 1) * LANES)
-                        old = state[v, x + 1, h, inside, :]
-                        state[v, x + 1, h, inside, :] = jnp.where(hit[:, side], value[:, side], old)
-
-            def outer(i, carry):
-                place(i * edge)
-                return carry
-
-            lax.fori_loop(0, 2, outer, 0)
+            def place(planes):
+                for x, (value, hit) in zip(planes, place_planes(planes, width_y, row_hot, z_hot, spread)):
+                    for v in range(nvar):
+                        for h in range(halves):
+                            side = slice(h * LANES, (h + 1) * LANES)
+                            old = state[v, x + 1, h, inside, :]
+                            state[v, x + 1, h, inside, :] = jnp.where(hit[:, side], value[v][:, side], old)
+
+            place((0, edge))
             for c in range(chunks):
                 start(sub + 1, 0, c)
 
-            def inner(x, carry):
-                place(x)
+            def inner(i, carry):
+                place((2 * i + 1, 2 * i + 2))
                 return carry
 
-            lax.fori_loop(1, edge, inner, 0)
+            lax.fori_loop(0, (rows - 2) // 2, inner, 0)
     for sub in range(SUBITERS):
         for d in range(1, comps):
             value_copy(sub, d).wait_send()
@@ -473,9 +564,13 @@
         pltpu.VMEM((pairs, points), BF16),
         pltpu.VMEM((width_z, points), BF16),
         pltpu.VMEM((2 * nvar, 2 * SUB, points), BF16),
-        pltpu.VMEM(((2 * nvar + 1) * width_y, points), BF16),
+        pltpu.VMEM((comps * slots, width_z, 2 * tile), BF16),
+        pltpu.VMEM((comps * slots, pairs, 2 * tile), F32),
+        pltpu.VMEM((comps * slots, nvar, SUB, 2 * tile), F32),
+        pltpu.VMEM((SUBITERS, 3, chunks // 2, nvar, halves, SUB, LANES), F32),
         dma((6 * halves,)),
         dma((SUBITERS, 3, 2, chunks)), dma((SUBITERS, 3, 2, chunks)),
+        dma((SUBITERS, 3, chunks // 2)), dma((SUBITERS, 3, chunks // 2)),
         dma((comps,)), dma((comps,)),
         dma((SUBITERS, comps)), dma((SUBITERS, comps)),
         dma((halves,)),
@@ -497,30 +592,29 @@
     )(jac, live, now, prev, kappa, donor, weights, recv)
 
 
-def finish_kernel(shift, state_ref, cells_ref, value_ref, out_ref, row_hot, z_hot, spread, placed):
-    nvar, _, width_y, width_z = state_ref.shape
-    x = pl.program_id(0)
-
-    @pl.when(x == 0)
+def finish_kernel(shift, state_ref, cells_ref, value_ref, out_ref, row_hot, z_hot, spread):
+    nvar, together, width_y, width_z = state_ref.shape
+    step = pl.program_id(0)
+
+    @pl.when(step == 0)
     def _():
         fill_hots(cells_ref, row_hot, z_hot, shift)
         fill_values(value_ref, spread)
 
-    part = place_plane(x, row_hot, z_hot, spread, placed)
-    hit = part[2 * nvar * width_y :, :] > 0.5
-    for v in range(nvar):
-        value = part[v * width_y : (v + 1) * width_y] + part[(nvar + v) * width_y : (nvar + v + 1) * width_y]
-        out_ref[v, 0] = jnp.where(hit, value, state_ref[v, 0])
+    planes = [step * together + i for i in range(together)]
+    for i, (value, hit) in enumerate(place_planes(planes, width_y, row_hot, z_hot, spread)):
+        for v in range(nvar):
+            out_ref[v, i] = jnp.where(hit, value[v], state_ref[v, i])
 
 
 def run_finish(state, cells, values):
     nvar, rows, width_y, width_z = state.shape
     points = cells.shape[0] * cells.shape[1]
-    block = pl.BlockSpec((nvar, 1, width_y, width_z), lambda x: (0, x, 0, 0))
+    block = pl.BlockSpec((nvar, 2, width_y, width_z), lambda x: (0, x, 0, 0))
     vmem = pl.BlockSpec(memory_space=pltpu.VMEM)
     return pl.pallas_call(
         functools.partial(finish_kernel, width_z.bit_length() - 1),
-        grid=(rows,),
+        grid=(rows // 2,),
         out_shape=jax.ShapeDtypeStruct(state.shape, F32),
         in_specs=[block, vmem, vmem],
         out_specs=block,
@@ -528,7 +622,6 @@
             pltpu.VMEM((rows * width_y, points), BF16),
             pltpu.VMEM((width_z, points), BF16),
             pltpu.VMEM((2 * nvar, 2 * SUB, points), BF16),
-            pltpu.VMEM(((2 * nvar + 1) * width_y, points), BF16),
         ],
         compiler_params=pltpu.CompilerParams(vmem_limit_bytes=VMEM_LIMIT),
         name="finish",

time: 97.3 us -> 84.4 us (0.87)
  the two profiles are of different devices: /device:TPU:2 before, /device:TPU:0 now
where the time goes in v2:
time: 84.4 us; the launch traced here: 84.1 us
  Pallas kernels  82.8 us (98%)
  local copies, waits for them, and re-layouts  1.3 us (2%)
    pallas_call x1, Pallas kernels, run_main(): pl.pallas_call(functools.partial(main_kernel, count, comps), out_shape=[j...  75.6 us
    pallas_call x1, Pallas kernels, run_finish(): pl.pallas_call(functools.partial(finish_kernel, width_z.bit_length() - 1)...  7.18 us

profile of v2, /device:TPU:0, one launch (start us, length us, event | category | flops | bytes accessed | tf_op | source)
XLA Modules:
  0.0 84.1 jit_solution(14042246912639161178)
XLA Ops:
  0.0 1.3 %copy.11 = f32[1,3,6,6]{3,2,0,1:T(8,128)} copy(f32[1,3,6,6]{3,0,2,1:T(1,128)} %param.11) | data formatting | bytes 864
  1.3 75.6 %subiterate.1 = (f32[6,8,32,256]{3,2,1,0:T(8,128)}, f32[8,2,6,128]{3,2,1,0:T(8,128)}, s32[16,128]{1,0:T(8,128)}) custom-call(f32[3,6,6]{2,1,0:T(8,128)} %bitcast.16, s32[8,8]{1,0:T(8,128)} %bitcast.18, f32[6,8,32,256]{3,2,1,0:T(8,128)} %bitcast.11, f32[6,8,32,256]{3,2,1,0:T(8,128)} %bitcast.12, f32[8,32,256]{2,1,0:T(8,128)} %bitcast.13, ...), custom_call_target="tpu_custom_call" | custom-call | tf_op jit(solution)/shard_map/subiterate/pallas_call | solution.py:578
  76.9 7.2 %finish.1 = f32[6,8,32,256]{3,2,1,0:T(8,128)} custom-call(f32[6,8,32,256]{3,2,1,0:T(8,128)} %get-tuple-element.8.state_ref, s32[16,128]{1,0:T(8,128)} %get-tuple-element.9.cells_ref, f32[8,2,6,128]{3,2,1,0:T(8,128)} %get-tuple-element.10.value_ref), custom_call_target="tpu_custom_call" | custom-call | tf_op jit(solution)/shard_map/finish/pallas_call | solution.py:615
